TPU v7x, 32 devices: a whole 2x2x4 slice. The times are simulated.
32 devices in a mesh: row: 4 (over y, x), col: 8 (over z, core).
Axes of the slice: x: 2, y: 2, z: 4, core: 2. Of those that a mesh axis runs over, the one named last changes fastest.
Arguments:
- right_side: bfloat16 [4, 8, 8, 128, 256], P('row', 'col'), may hold values from -6 to 6
- diag_inverse: bfloat16 [4, 8, 8, 128, 128], P('row', 'col'), may hold values from -0.5 to 0.5
- panels: bfloat16 [7, 4, 400, 128, 128], P(None, 'row', 'col'), may hold values from -0.0546875 to 0.0546875
- tile_source: int32 [7, 4, 400], P(None, 'row', 'col'), may hold values from 0 to 3
- tile_target: int32 [7, 4, 400], P(None, 'row', 'col'), may hold values from 0 to 7
Outputs:
- solution: float32 [4, 8, 8, 128, 256], P('row', 'col')
All inputs are finite; a program needn't handle non-finite values.
Results may differ from a plain program's by a relative error of at most 0.017.
Values may be sent and summed in bfloat16 or wider, within the bound.
A program may use at most 128 MiB of HBM per device.

v0:
```python
import jax
import jax.numpy as jnp
from jax import lax
from jax.sharding import PartitionSpec as P


def local_update(segment, panel, source, target):
    columns = lax.axis_size("col")
    picked = jnp.take(segment, source, axis=0)
    prods = jnp.einsum("qab,qbc->qac", panel, picked, preferred_element_type=jnp.float32)
    onehot = (target[None, :] == jnp.arange(columns, dtype=jnp.int32)[:, None]).astype(jnp.float32)
    sums = jnp.dot(onehot, prods.reshape(prods.shape[0], -1), precision=lax.Precision.HIGHEST)
    return sums.reshape(columns, prods.shape[1], prods.shape[2]).astype(jnp.bfloat16)


def advance_whole(block, panel, source, target):
    segment = lax.all_gather(block.astype(jnp.bfloat16)[None], "row", axis=0, tiled=True)
    partial_value = local_update(segment, panel, source, target)
    return lax.psum_scatter(partial_value, "col", scatter_dimension=0, tiled=True).astype(
        jnp.float32
    )[0]


def local(right_side, diag_inverse, panels, tile_source, tile_target):
    sections = right_side.shape[2]
    width = right_side.shape[4]
    bounds = [(0, width)]
    incoming = [None for bound in bounds]
    solved = []
    for section in range(sections):
        lower, upper = bounds[0]
        current = right_side[0, 0, section, :, lower:upper].astype(jnp.float32)
        if section > 0:
            current = current - incoming[0]
        block = jnp.dot(
            diag_inverse[0, 0, section],
            current.astype(jnp.bfloat16),
            preferred_element_type=jnp.float32,
        )
        if section + 1 < sections:
            incoming[0] = advance_whole(
                block, panels[section, 0], tile_source[section, 0], tile_target[section, 0]
            )
        solved.append(block)
    return jnp.stack(solved, axis=0)[None, None]


def solution(mesh):
    return jax.shard_map(
        local,
        mesh=mesh,
        in_specs=(
            P("row", "col", None, None, None),
            P("row", "col", None, None, None),
            P(None, "row", "col", None, None),
            P(None, "row", "col"),
            P(None, "row", "col"),
        ),
        out_specs=P("row", "col", None, None, None),
        check_vma=False,
    )
```

profile of v0, /device:TPU:0, one launch (start us, length us, event | category | flops | bytes accessed | tf_op | source)
XLA Modules:
  0.0 471.4 jit_solution(18376820517892712203)
XLA Ops:
  8.2 10.5 %all-gather = bf16[512,256]{1,0:T(8,128)(2,1)S(1)} all-gather(bf16[128,256]{1,0:T(8,128)(2,1)S(1)} %get-tuple-element.40), channel_id=2, replica_groups=mesh['row'=4,'col'=8] {'row'}, dimensions={0}, use_global_device_ids=true | all-gather | bytes 327680 | tf_op jit(solution)/shard_map/all_gather | solution.py:17
  26.1 8.2 %copy.56 = f32[50,128,256]{2,1,0:T(8,128)} copy(f32[50,128,256]{1,2,0:T(8,128)} %fusion.35) | data formatting | bytes 13107200 | tf_op jit(solution)/shard_map/qab,qbc->qac/dot_general | solution.py:10
  38.1 6.1 %fusion.77 = bf16[8,128,256]{2,0,1:T(8,128)(2,1)S(1)} fusion(f32[128,256,50]{1,0,2:T(8,128)S(1)} %slice_bitcast_fusion.6, s32[50]{0:T(128)S(1)} %get-tuple-element.25), kind=kOutput, calls=%fused_computation.77 | convolution fusion | flops 157548944 | bytes 7078088 | tf_op jit(solution)/shard_map/dot_general | solution.py:12
  45.2 31.7 %reduce-scatter.8.cloned.1.call-done = bf16[1,128,256]{2,1,0:T(8,128)(2,1)} async-done(((bf16[8,128,256]{2,1,0:T(8,128)(2,1)}), bf16[1,128,256]{2,1,0:T(8,128)(2,1)}) %reduce-scatter.8.cloned.1.call-update) | async-done | bytes 65552 | tf_op jit(solution)/shard_map/reduce_scatter | solution.py:19
  78.6 9.0 %all-gather.1 = bf16[512,256]{1,0:T(8,128)(2,1)S(1)} all-gather(bf16[128,256]{1,0:T(8,128)(2,1)S(1)} %bitcast.364), channel_id=3, replica_groups=mesh['row'=4,'col'=8] {'row'}, dimensions={0}, use_global_device_ids=true | all-gather | bytes 327680 | tf_op jit(solution)/shard_map/all_gather | solution.py:17
  88.4 5.3 %fusion.38 = f32[50,128,256]{1,2,0:T(8,128)} fusion(bf16[50,128,256]{2,1,0:T(8,128)(2,1)S(1)} %gather_fusion.1, pred[50]{0:T(512)(128)(4,1)} %get-tuple-element.33, bf16[7,1,50,128,128]{4,3,2,1,0:T(8,128)(2,1)} %param.9), kind=kOutput, calls=%fused_computation.50 | convolution fusion | flops 421068800 | bytes 11469312 | tf_op jit(solution)/shard_map/qab,qbc->qac/dot_general | solution.py:10
  93.7 8.2 %copy.61 = f32[50,128,256]{2,1,0:T(8,128)} copy(f32[50,128,256]{1,2,0:T(8,128)} %fusion.38) | data formatting | bytes 13107200 | tf_op jit(solution)/shard_map/qab,qbc->qac/dot_general | solution.py:10
  105.2 6.1 %fusion.80 = bf16[8,128,256]{2,0,1:T(8,128)(2,1)S(1)} fusion(f32[128,256,50]{1,0,2:T(8,128)S(1)} %slice_bitcast_fusion.5, s32[50]{0:T(128)S(1)} %copy-done.3), kind=kOutput, calls=%fused_computation.78 | convolution fusion | flops 157548944 | bytes 7078088 | tf_op jit(solution)/shard_map/dot_general | solution.py:12
  112.3 28.8 %reduce-scatter.10.cloned.1.call-done = bf16[1,128,256]{2,1,0:T(8,128)(2,1)} async-done(((bf16[8,128,256]{2,1,0:T(8,128)(2,1)}), bf16[1,128,256]{2,1,0:T(8,128)(2,1)}) %reduce-scatter.10.cloned.1.call-update) | async-done | bytes 65552 | tf_op jit(solution)/shard_map/reduce_scatter | solution.py:19
  142.8 9.5 %all-gather.2 = bf16[512,256]{1,0:T(8,128)(2,1)S(1)} all-gather(bf16[128,256]{1,0:T(8,128)(2,1)S(1)} %bitcast.365), channel_id=4, replica_groups=mesh['row'=4,'col'=8] {'row'}, dimensions={0}, use_global_device_ids=true | all-gather | bytes 327680 | tf_op jit(solution)/shard_map/all_gather | solution.py:17
  153.0 5.3 %fusion.41 = f32[50,128,256]{1,2,0:T(8,128)} fusion(bf16[50,128,256]{2,1,0:T(8,128)(2,1)S(1)} %gather_fusion.2, pred[50]{0:T(512)(128)(4,1)} %get-tuple-element.31, bf16[7,1,50,128,128]{4,3,2,1,0:T(8,128)(2,1)} %param.9), kind=kOutput, calls=%fused_computation.51 | convolution fusion | flops 421068800 | bytes 11469312 | tf_op jit(solution)/shard_map/qab,qbc->qac/dot_general | solution.py:10
  158.3 8.2 %copy.66 = f32[50,128,256]{2,1,0:T(8,128)} copy(f32[50,128,256]{1,2,0:T(8,128)} %fusion.41) | data formatting | bytes 13107200 | tf_op jit(solution)/shard_map/qab,qbc->qac/dot_general | solution.py:10
  169.8 6.1 %fusion.83 = bf16[8,128,256]{2,0,1:T(8,128)(2,1)S(1)} fusion(f32[128,256,50]{1,0,2:T(8,128)S(1)} %slice_bitcast_fusion.4, s32[50]{0:T(128)S(1)} %copy-done.2), kind=kOutput, calls=%fused_computation.79 | convolution fusion | flops 157548944 | bytes 7078088 | tf_op jit(solution)/shard_map/dot_general | solution.py:12
  176.9 28.7 %reduce-scatter.12.cloned.1.call-done = bf16[1,128,256]{2,1,0:T(8,128)(2,1)} async-done(((bf16[8,128,256]{2,1,0:T(8,128)(2,1)}), bf16[1,128,256]{2,1,0:T(8,128)(2,1)}) %reduce-scatter.12.cloned.1.call-update) | async-done | bytes 65552 | tf_op jit(solution)/shard_map/reduce_scatter | solution.py:19
  207.4 8.9 %all-gather.3 = bf16[512,256]{1,0:T(8,128)(2,1)S(1)} all-gather(bf16[128,256]{1,0:T(8,128)(2,1)S(1)} %bitcast.366), channel_id=5, replica_groups=mesh['row'=4,'col'=8] {'row'}, dimensions={0}, use_global_device_ids=true | all-gather | bytes 327680 | tf_op jit(solution)/shard_map/all_gather | solution.py:17
  217.1 5.3 %fusion.44 = f32[50,128,256]{1,2,0:T(8,128)} fusion(bf16[50,128,256]{2,1,0:T(8,128)(2,1)S(1)} %gather_fusion.3, pred[50]{0:T(512)(128)(4,1)} %get-tuple-element.29, bf16[7,1,50,128,128]{4,3,2,1,0:T(8,128)(2,1)} %param.9), kind=kOutput, calls=%fused_computation.52 | convolution fusion | flops 421068800 | bytes 11469312 | tf_op jit(solution)/shard_map/qab,qbc->qac/dot_general | solution.py:10
  222.4 8.2 %copy.71 = f32[50,128,256]{2,1,0:T(8,128)} copy(f32[50,128,256]{1,2,0:T(8,128)} %fusion.44) | data formatting | bytes 13107200 | tf_op jit(solution)/shard_map/qab,qbc->qac/dot_general | solution.py:10
  233.9 6.1 %fusion.86 = bf16[8,128,256]{2,0,1:T(8,128)(2,1)S(1)} fusion(f32[128,256,50]{1,0,2:T(8,128)S(1)} %slice_bitcast_fusion.3, s32[50]{0:T(128)S(1)} %copy-done.1), kind=kOutput, calls=%fused_computation.80 | convolution fusion | flops 157548944 | bytes 7078088 | tf_op jit(solution)/shard_map/dot_general | solution.py:12
  241.0 28.8 %reduce-scatter.14.cloned.1.call-done = bf16[1,128,256]{2,1,0:T(8,128)(2,1)} async-done(((bf16[8,128,256]{2,1,0:T(8,128)(2,1)}), bf16[1,128,256]{2,1,0:T(8,128)(2,1)}) %reduce-scatter.14.cloned.1.call-update) | async-done | bytes 65552 | tf_op jit(solution)/shard_map/reduce_scatter | solution.py:19
  271.5 9.3 %all-gather.4 = bf16[512,256]{1,0:T(8,128)(2,1)S(1)} all-gather(bf16[128,256]{1,0:T(8,128)(2,1)S(1)} %bitcast.367), channel_id=6, replica_groups=mesh['row'=4,'col'=8] {'row'}, dimensions={0}, use_global_device_ids=true | all-gather | bytes 327680 | tf_op jit(solution)/shard_map/all_gather | solution.py:17
  281.6 5.3 %fusion.47 = f32[50,128,256]{1,2,0:T(8,128)} fusion(bf16[50,128,256]{2,1,0:T(8,128)(2,1)S(1)} %gather_fusion.4, pred[50]{0:T(512)(128)(4,1)} %get-tuple-element.27, bf16[7,1,50,128,128]{4,3,2,1,0:T(8,128)(2,1)} %param.9), kind=kOutput, calls=%fused_computation.53 | convolution fusion | flops 421068800 | bytes 11469312 | tf_op jit(solution)/shard_map/qab,qbc->qac/dot_general | solution.py:10
  286.8 8.2 %copy.76 = f32[50,128,256]{2,1,0:T(8,128)} copy(f32[50,128,256]{1,2,0:T(8,128)} %fusion.47) | data formatting | bytes 13107200 | tf_op jit(solution)/shard_map/qab,qbc->qac/dot_general | solution.py:10
  298.3 6.1 %fusion.89 = bf16[8,128,256]{2,0,1:T(8,128)(2,1)S(1)} fusion(f32[128,256,50]{1,0,2:T(8,128)S(1)} %slice_bitcast_fusion.2, s32[50]{0:T(128)S(1)} %get-tuple-element.21), kind=kOutput, calls=%fused_computation.81 | convolution fusion | flops 157548944 | bytes 7078088 | tf_op jit(solution)/shard_map/dot_general | solution.py:12
  305.5 28.5 %reduce-scatter.16.cloned.1.call-done = bf16[1,128,256]{2,1,0:T(8,128)(2,1)} async-done(((bf16[8,128,256]{2,1,0:T(8,128)(2,1)}), bf16[1,128,256]{2,1,0:T(8,128)(2,1)}) %reduce-scatter.16.cloned.1.call-update) | async-done | bytes 65552 | tf_op jit(solution)/shard_map/reduce_scatter | solution.py:19
  335.6 9.2 %all-gather.5 = bf16[512,256]{1,0:T(8,128)(2,1)S(1)} all-gather(bf16[128,256]{1,0:T(8,128)(2,1)S(1)} %bitcast.368), channel_id=7, replica_groups=mesh['row'=4,'col'=8] {'row'}, dimensions={0}, use_global_device_ids=true | all-gather | bytes 327680 | tf_op jit(solution)/shard_map/all_gather | solution.py:17
  350.9 8.2 %copy.81 = f32[50,128,256]{2,1,0:T(8,128)} copy(f32[50,128,256]{1,2,0:T(8,128)} %fusion.50) | data formatting | bytes 13107200 | tf_op jit(solution)/shard_map/qab,qbc->qac/dot_general | solution.py:10
  362.4 6.1 %fusion.92 = bf16[8,128,256]{2,0,1:T(8,128)(2,1)S(1)} fusion(f32[128,256,50]{1,0,2:T(8,128)S(1)} %slice_bitcast_fusion.1, s32[50]{0:T(128)S(1)} %get-tuple-element.26), kind=kOutput, calls=%fused_computation.82 | convolution fusion | flops 157548944 | bytes 7078088 | tf_op jit(solution)/shard_map/dot_general | solution.py:12
  369.5 28.6 %reduce-scatter.18.cloned.1.call-done = bf16[1,128,256]{2,1,0:T(8,128)(2,1)} async-done(((bf16[8,128,256]{2,1,0:T(8,128)(2,1)}), bf16[1,128,256]{2,1,0:T(8,128)(2,1)}) %reduce-scatter.18.cloned.1.call-update) | async-done | bytes 65552 | tf_op jit(solution)/shard_map/reduce_scatter | solution.py:19
  399.8 9.7 %all-gather.6 = bf16[512,256]{1,0:T(8,128)(2,1)S(1)} all-gather(bf16[128,256]{1,0:T(8,128)(2,1)S(1)} %bitcast.369), channel_id=8, replica_groups=mesh['row'=4,'col'=8] {'row'}, dimensions={0}, use_global_device_ids=true | all-gather | bytes 327680 | tf_op jit(solution)/shard_map/all_gather | solution.py:17
  415.6 8.2 %copy.86 = f32[50,128,256]{2,1,0:T(8,128)} copy(f32[50,128,256]{1,2,0:T(8,128)} %fusion.53) | data formatting | bytes 13107200 | tf_op jit(solution)/shard_map/qab,qbc->qac/dot_general | solution.py:10
  427.0 6.1 %fusion.95 = bf16[8,128,256]{2,0,1:T(8,128)(2,1)S(1)} fusion(f32[128,256,50]{1,0,2:T(8,128)S(1)} %slice_bitcast_fusion, s32[50]{0:T(128)S(1)} %get-tuple-element.20), kind=kOutput, calls=%fused_computation.83 | convolution fusion | flops 157548944 | bytes 7078088 | tf_op jit(solution)/shard_map/dot_general | solution.py:12
  434.1 28.7 %reduce-scatter.20.cloned.1.call-done = bf16[1,128,256]{2,1,0:T(8,128)(2,1)} async-done(((bf16[8,128,256]{2,1,0:T(8,128)(2,1)}), bf16[1,128,256]{2,1,0:T(8,128)(2,1)}) %reduce-scatter.20.cloned.1.call-update) | async-done | bytes 65552 | tf_op jit(solution)/shard_map/reduce_scatter | solution.py:19
  (79 shorter events, 66.4 us)
Async XLA Ops:
  6.5 70.4 %reduce-scatter.8.cloned.1.call-start = ((), (), s32[]{:S(2)}) async-start(), calls=%async_computation.7 | async-start | bytes 589824 | tf_op jit(solution)/shard_map/reduce_scatter | solution.py:19
  34.3 3.3 copy-start
  37.6 7.6 %copy-start.11 = (s32[50]{0:T(128)S(1)}, s32[50]{0:T(128)}, u32[]{:S(2)}) copy-start(s32[50]{0:T(128)} %get-tuple-element.34) | copy-start | bytes 604
  45.2 95.9 %reduce-scatter.10.cloned.1.call-start = ((), (), s32[]{:S(2)}) async-start(), calls=%async_computation.8 | async-start | bytes 589824 | tf_op jit(solution)/shard_map/reduce_scatter | solution.py:19
  101.9 3.3 copy-start.3
  105.2 7.1 %copy-start.10 = (s32[50]{0:T(128)S(1)}, s32[50]{0:T(128)}, u32[]{:S(2)}) copy-start(s32[50]{0:T(128)} %get-tuple-element.32) | copy-start | bytes 604
  112.3 93.4 %reduce-scatter.12.cloned.1.call-start = ((), (), s32[]{:S(2)}) async-start(), calls=%async_computation.9 | async-start | bytes 589824 | tf_op jit(solution)/shard_map/reduce_scatter | solution.py:19
  166.5 3.3 copy-start.2
  169.8 7.1 %copy-start.9 = (s32[50]{0:T(128)S(1)}, s32[50]{0:T(128)}, u32[]{:S(2)}) copy-start(s32[50]{0:T(128)} %get-tuple-element.30) | copy-start | bytes 604
  176.9 92.9 %reduce-scatter.14.cloned.1.call-start = ((), (), s32[]{:S(2)}) async-start(), calls=%async_computation.10 | async-start | bytes 589824 | tf_op jit(solution)/shard_map/reduce_scatter | solution.py:19
  230.6 3.3 copy-start.1
  233.9 7.1 %copy-start.8 = (s32[50]{0:T(128)S(1)}, s32[50]{0:T(128)}, u32[]{:S(2)}) copy-start(s32[50]{0:T(128)} %get-tuple-element.28) | copy-start | bytes 604
  240.9 93.0 %reduce-scatter.16.cloned.1.call-start = ((), (), s32[]{:S(2)}) async-start(), calls=%async_computation.11 | async-start | bytes 589824 | tf_op jit(solution)/shard_map/reduce_scatter | solution.py:19
  298.3 7.1 %copy-start.7 = (s32[50]{0:T(128)S(1)}, s32[50]{0:T(128)}, u32[]{:S(2)}) copy-start(s32[50]{0:T(128)} %get-tuple-element.38) | copy-start | bytes 604
  304.4 41.2 %copy-start.5 = (pred[50]{0:T(512)(128)(4,1)S(1)}, pred[50]{0:T(512)(128)(4,1)}, u32[]{:S(2)}) copy-start(pred[50]{0:T(512)(128)(4,1)} %get-tuple-element.37) | copy-start | bytes 154
  305.4 92.7 %reduce-scatter.18.cloned.1.call-start = ((), (), s32[]{:S(2)}) async-start(), calls=%async_computation.12 | async-start | bytes 589824 | tf_op jit(solution)/shard_map/reduce_scatter | solution.py:19
  362.4 7.1 %copy-start.6 = (s32[50]{0:T(128)S(1)}, s32[50]{0:T(128)}, u32[]{:S(2)}) copy-start(s32[50]{0:T(128)} %get-tuple-element.7) | copy-start | bytes 604
  362.4 47.8 %copy-start.4 = (pred[50]{0:T(512)(128)(4,1)S(1)}, pred[50]{0:T(512)(128)(4,1)}, u32[]{:S(2)}) copy-start(pred[50]{0:T(512)(128)(4,1)} %get-tuple-element.6) | copy-start | bytes 154
  369.5 93.3 %reduce-scatter.20.cloned.1.call-start = ((), (), s32[]{:S(2)}) async-start(), calls=%async_computation.13 | async-start | bytes 589824 | tf_op jit(solution)/shard_map/reduce_scatter | solution.py:19
Sparse Core Ops, SparseCore 0:
  45.3 31.5 reduce-scatter.7
  112.4 28.6 reduce-scatter.9
  177.0 28.6 reduce-scatter.11
  241.1 28.6 reduce-scatter.13
  305.5 28.3 reduce-scatter.15
  369.6 28.4 reduce-scatter.17
  434.2 28.5 reduce-scatter.19
where the time goes:
time: 480 us; the launch traced here: 471 us
  waiting for transfers between devices  204 us (42%)
  matrix products  93.2 us (19%)
  local copies, waits for them, and re-layouts  92.6 us (19%)
  blocking collectives  66.1 us (14%)
  between operations  14 us (3%)
    reduce_scatter x7, waiting for transfers between devices, advance_whole(): lax.psum_scatter(partial_value, 'col', scatter_dimension=0, tiled=True)  204 us
    all_gather x7, blocking collectives, advance_whole(): lax.all_gather(block.astype(jnp.bfloat16)[None], 'row', axis=0, tiled=True)  66.1 us
    dot_general x7, local copies, waits for them, and re-layouts, local_update(): jnp.einsum('qab,qbc->qac', panel, picked, preferred_element_type=jnp.floa...  57.4 us
    dot_general x7, matrix products, local_update(): jnp.dot(onehot, prods.reshape(prods.shape[0], -1), precision=lax.Precisio...  42.7 us
    dot_general x7, matrix products, local_update(): jnp.einsum('qab,qbc->qac', panel, picked, preferred_element_type=jnp.floa...  37 us
    dot_general x7, local copies, waits for them, and re-layouts, local_update(): jnp.dot(onehot, prods.reshape(prods.shape[0], -1), precision=lax.Precisio...  23 us
    dot_general x8, matrix products, local(): jnp.dot(diag_inverse[0, 0, section], current.astype(jnp.bfloat16), prefer...  13.5 us
  transfers between devices with their start and end apart: 7, of which 7 were waited for; matrix products, arithmetic and copies ran while one was open for 0% of the time, Pallas kernels for 0%

commit v1 on v0

v1 whole, which is shorter than its diff:
```python
import functools

import jax
import jax.numpy as jnp
from jax import lax
from jax.experimental import pallas as pl
from jax.experimental.pallas import tpu as pltpu
from jax.sharding import PartitionSpec as P

MESH = pl.DeviceIdType.MESH


def fold_kernel(rows, cols, source_ref, target_ref, panel_ref, out_ref, acc):
    level = pl.program_id(0)
    tiles, block = panel_ref.shape[2], panel_ref.shape[3]
    acc[...] = jnp.zeros_like(acc)

    def add(q, carry):
        target = target_ref[level, q]
        place = (target & 1) * (cols // 2) + (target >> 1)
        row = pl.multiple_of(place * block, block)
        column = pl.multiple_of(source_ref[level, q] * block, block)
        acc[pl.ds(row, block), pl.ds(column, block)] += panel_ref[0, 0, q].astype(jnp.float32)
        return carry

    lax.fori_loop(0, tiles, add, 0)
    out_ref[0] = acc[...].astype(out_ref.dtype)


def fold(panels, tile_source, tile_target, rows, cols):
    levels, _, tiles, block, _ = panels.shape
    return pl.pallas_call(
        functools.partial(fold_kernel, rows, cols),
        out_shape=jax.ShapeDtypeStruct((levels, cols * block, rows * block), jnp.bfloat16),
        grid_spec=pltpu.PrefetchScalarGridSpec(
            num_scalar_prefetch=2,
            grid=(levels,),
            in_specs=[pl.BlockSpec((1, 1, tiles, block, block), lambda s, *_: (s, 0, 0, 0, 0))],
            out_specs=pl.BlockSpec((1, cols * block, rows * block), lambda s, *_: (s, 0, 0)),
            scratch_shapes=[pltpu.VMEM((cols * block, rows * block), jnp.float32)],
        ),
        compiler_params=pltpu.CompilerParams(vmem_limit_bytes=56 * 1024 * 1024),
    )(tile_source[:, 0], tile_target[:, 0], panels)


def solve_kernel(rows, cols, window, right_ref, diag_ref, matrix_ref, out_ref,
                 matrix, gathered, pair_out, pair_in, own, shard_out, shard_in,
                 matrix_sem, gather_send, gather_recv, pair_send, pair_recv, shard_send, shard_recv):
    sections, block, width = right_ref.shape
    levels = sections - 1
    halves = gathered.shape[1]
    part = width // halves
    chips = cols // 2
    i, j = lax.axis_index("row"), lax.axis_index("col")
    z, core = j // 2, j % 2

    def row_peer(d):
        return (lax.rem(i + d, rows), j)

    def chip_peer(d):
        return (i, lax.rem(z + d, chips) * 2 + core)

    sibling = (i, z * 2 + 1 - core)

    def load(s):
        return pltpu.make_async_copy(matrix_ref.at[s], matrix.at[s % window], matrix_sem.at[s % window])

    for s in range(min(window, levels)):
        load(s).start()

    barrier = pltpu.get_barrier_semaphore()
    peers = [row_peer(d) for d in range(1, rows)] + [sibling] + [chip_peer(d) for d in range(1, chips)]
    for peer in peers:
        pl.semaphore_signal(barrier, inc=1, device_id=peer, device_id_type=MESH)
    pl.semaphore_wait(barrier, len(peers))

    def block_of(index):
        return pl.ds(pl.multiple_of(index * block, block), block)

    def gather_copy(p, h, d):
        here = gathered.at[p, h, block_of(i)]
        return pltpu.make_async_remote_copy(
            src_ref=here, dst_ref=here, send_sem=gather_send.at[p, h, d - 1], recv_sem=gather_recv.at[p, h, d - 1],
            device_id=row_peer(d), device_id_type=MESH)

    def pair_copy(p, h):
        return pltpu.make_async_remote_copy(
            src_ref=pair_out.at[p, h], dst_ref=pair_in.at[p, h], send_sem=pair_send.at[p, h],
            recv_sem=pair_recv.at[p, h], device_id=sibling, device_id_type=MESH)

    def shard_copy(p, h, d):
        return pltpu.make_async_remote_copy(
            src_ref=shard_out.at[p, h, block_of(lax.rem(z + d, chips))], dst_ref=shard_in.at[p, h, d - 1],
            send_sem=shard_send.at[p, h, d - 1], recv_sem=shard_recv.at[p, h, d - 1],
            device_id=chip_peer(d), device_id_type=MESH)

    def finish(s, h, incoming):
        columns = pl.ds(h * part, part)
        current = right_ref[s, :, columns].astype(jnp.float32)
        if incoming is not None:
            current = current - incoming
        solved = jnp.dot(diag_ref[s], current.astype(jnp.bfloat16), preferred_element_type=jnp.float32)
        out_ref[s, :, columns] = solved
        return solved.astype(jnp.bfloat16)

    def spread(s, h, segment):
        p = s % 2
        gathered[p, h, block_of(i), :] = segment
        for d in range(1, rows):
            gather_copy(p, h, d).start()

    def update(s, h):
        p = s % 2
        for d in range(1, rows):
            gather_copy(p, h, d).wait_recv()
        segment = gathered[p, h]
        tall = chips * block
        other = pl.ds(pl.multiple_of((1 - core) * tall, tall), tall)
        mine = pl.ds(pl.multiple_of(core * tall, tall), tall)
        pair_out[p, h] = jnp.dot(
            matrix[s % window, other, :], segment, preferred_element_type=jnp.float32).astype(jnp.bfloat16)
        pair_copy(p, h).start()
        own[h] = jnp.dot(matrix[s % window, mine, :], segment, preferred_element_type=jnp.float32)

    def combine(s, h):
        p = s % 2
        pair_copy(p, h).wait_recv()
        total = own[h] + pair_in[p, h].astype(jnp.float32)
        own[h] = total
        shard_out[p, h] = total.astype(jnp.bfloat16)
        for d in range(1, chips):
            shard_copy(p, h, d).start()

    def incoming_of(s, h):
        p = s % 2
        total = own[h, block_of(z), :]
        for d in range(1, chips):
            shard_copy(p, h, d).wait_recv()
        for d in range(1, chips):
            total = total + shard_in[p, h, d - 1].astype(jnp.float32)
        return total

    def drain(s, h):
        p = s % 2
        for d in range(1, rows):
            gather_copy(p, h, d).wait_send()
        pair_copy(p, h).wait_send()
        for d in range(1, chips):
            shard_copy(p, h, d).wait_send()

    def advance(s, last):
        load(s).wait()
        for h in range(halves):
            update(s, h)
        for h in range(halves):
            combine(s, h)
        if window < levels and not last:
            @pl.when(s + window < levels)
            def _():
                load(s + window).start()
        for h in range(halves):
            segment = finish(s + 1, h, incoming_of(s, h))
            if not last:
                spread(s + 1, h, segment)
        for h in range(halves):
            drain(s, h)

    for h in range(halves):
        spread(0, h, finish(0, h, None))

    def step(s, carry):
        advance(s, False)
        return carry

    lax.fori_loop(0, levels - 1, step, 0)
    advance(levels - 1, True)


def local(right_side, diag_inverse, panels, tile_source, tile_target):
    rows, cols = lax.axis_size("row"), lax.axis_size("col")
    sections, block, width = right_side.shape[2:]
    levels = sections - 1
    halves = 2 if width % 256 == 0 else 1
    part = width // halves
    chips = cols // 2
    matrix = fold(panels, tile_source, tile_target, rows, cols)
    window = levels if levels * matrix[0].size * 2 <= 24 * 1024 * 1024 else 2
    dma = pltpu.SemaphoreType.DMA
    vmem = pl.BlockSpec(memory_space=pltpu.VMEM)
    solved = pl.pallas_call(
        functools.partial(solve_kernel, rows, cols, window),
        out_shape=jax.ShapeDtypeStruct((sections, block, width), jnp.float32),
        in_specs=[vmem, vmem, pl.BlockSpec(memory_space=pl.ANY)],
        out_specs=vmem,
        scratch_shapes=[
            pltpu.VMEM((window, cols * block, rows * block), jnp.bfloat16),
            pltpu.VMEM((2, halves, rows * block, part), jnp.bfloat16),
            pltpu.VMEM((2, halves, chips * block, part), jnp.bfloat16),
            pltpu.VMEM((2, halves, chips * block, part), jnp.bfloat16),
            pltpu.VMEM((halves, chips * block, part), jnp.float32),
            pltpu.VMEM((2, halves, chips * block, part), jnp.bfloat16),
            pltpu.VMEM((2, halves, chips - 1, block, part), jnp.bfloat16),
            dma((window,)),
            dma((2, halves, rows - 1)),
            dma((2, halves, rows - 1)),
            dma((2, halves)),
            dma((2, halves)),
            dma((2, halves, chips - 1)),
            dma((2, halves, chips - 1)),
        ],
        compiler_params=pltpu.CompilerParams(
            collective_id=0, has_side_effects=True, vmem_limit_bytes=56 * 1024 * 1024),
    )(right_side[0, 0], diag_inverse[0, 0], matrix)
    return solved[None, None]


def solution(mesh):
    return jax.shard_map(
        local,
        mesh=mesh,
        in_specs=(
            P("row", "col", None, None, None),
            P("row", "col", None, None, None),
            P(None, "row", "col", None, None),
            P(None, "row", "col"),
            P(None, "row", "col"),
        ),
        out_specs=P("row", "col", None, None, None),
        check_vma=False,
    )
```

time: 480 us -> 110 us (0.23); the launches traced: 471 us -> 109 us
  waiting for transfers between devices: 204 us -> 0 us
  Pallas kernels: 0 us -> 106 us
  matrix products: 93.2 us -> 0 us
  local copies, waits for them, and re-layouts: 92.6 us -> 3.57 us
  blocking collectives: 66.1 us -> 0 us
  between operations: 14 us -> 0.01 us
    reduce_scatter x7 -> x0, waiting for transfers between devices: 204 us -> none  [advance_whole(): lax.psum_scatter(partial_value, 'col', scatter_dimension=0, tiled=True)]
    pallas_call x0 -> x2, Pallas kernels: none -> 106 us  [the longest x1 91.9 us: local(): pl.pallas_call(functools.partial(solve_kernel, rows, cols, window), out_s...]
    dot_general x22 -> x0, matrix products: 93.2 us -> none  [the longest x7 42.7 us: local_update(): jnp.dot(onehot, prods.reshape(prods.shape[0], -1), precision=lax.Precisio...]
    dot_general x14 -> x0, local copies, waits for them, and re-layouts: 80.4 us -> none  [the longest x7 57.4 us: local_update(): jnp.einsum('qab,qbc->qac', panel, picked, preferred_element_type=jnp.floa...]
    all_gather x7 -> x0, blocking collectives: 66.1 us -> none  [advance_whole(): lax.all_gather(block.astype(jnp.bfloat16)[None], 'row', axis=0, tiled=True)]
    convert_element_type x7 -> x0, local copies, waits for them, and re-layouts: 6.34 us -> none  [local_update(): sums.reshape(columns, prods.shape[1], prods.shape[2]).astype(jnp.bfloat16)]
    gather x7 -> x0, local copies, waits for them, and re-layouts: 5.31 us -> none  [local_update(): picked = jnp.take(segment, source, axis=0)]
  transfers between devices with their start and end apart: 7 -> 0, of which waited for: 7 -> 0; matrix products, arithmetic and copies ran while one was open for 0% -> 0% of each run, Pallas kernels for 0% -> 0%
where the time goes in v1:
time: 110 us; the launch traced here: 109 us
  Pallas kernels  106 us (96%)
  local copies, waits for them, and re-layouts  3.57 us (3%)
    pallas_call x1, Pallas kernels, local(): pl.pallas_call(functools.partial(solve_kernel, rows, cols, window), out_s...  91.9 us
    pallas_call x1, Pallas kernels, fold(): pl.pallas_call(functools.partial(fold_kernel, rows, cols), out_shape=jax....  13.8 us
    unnamed x2, local copies, waits for them, and re-layouts  3.57 us

profile of v1, /device:TPU:0, one launch (start us, length us, event | category | flops | bytes accessed | tf_op | source)
XLA Modules:
  0.0 109.3 jit_solution(17585740164024577405)
XLA Ops:
  0.0 1.3 %copy_bitcast_fusion = (s32[7,50]{1,0:T(8,128)}, s32[7,50]{1,0:T(8,128)}) fusion(s32[7,1,50]{2,1,0:T(1,128)} %param.9, s32[7,1,50]{2,1,0:T(1,128)} %param.8), kind=kLoop, calls=%fused_computation | loop fusion | bytes 5600
  1.3 13.8 %shard_map.55.matrix_ref = bf16[7,1024,512]{2,1,0:T(8,128)(2,1)} custom-call(s32[7,50]{1,0:T(8,128)} %get-tuple-element.6.source_ref, s32[7,50]{1,0:T(8,128)} %get-tuple-element.5.target_ref, bf16[7,1,50,128,128]{4,3,2,1,0:T(8,128)(2,1)} %panel_ref.1), custom_call_target="tpu_custom_call" | custom-call | tf_op jit(solution)/shard_map/pallas_call | solution.py:32
  15.1 91.9 %shard_map.56 = f32[8,128,256]{2,1,0:T(8,128)} custom-call(bf16[8,128,256]{2,1,0:T(8,128)(2,1)} %bitcast.8, bf16[8,128,128]{2,1,0:T(8,128)(2,1)} %bitcast.9, bf16[7,1024,512]{2,1,0:T(8,128)(2,1)} %shard_map.55.matrix_ref), custom_call_target="tpu_custom_call" | custom-call | tf_op jit(solution)/shard_map/pallas_call | solution.py:190
  107.0 2.3 %copy.11 = f32[1,1,8,128,256]{4,3,2,1,0:T(8,128)} copy(f32[1,1,8,128,256]{4,3,2,1,0:T(8,128)} %bitcast.7) | data formatting | bytes 2097152

commit v2 on v1

--- a/solution.py
+++ b/solution.py
@@ -10,44 +10,25 @@
 MESH = pl.DeviceIdType.MESH
 
 
-def fold_kernel(rows, cols, source_ref, target_ref, panel_ref, out_ref, acc):
-    level = pl.program_id(0)
-    tiles, block = panel_ref.shape[2], panel_ref.shape[3]
-    acc[...] = jnp.zeros_like(acc)
-
-    def add(q, carry):
-        target = target_ref[level, q]
-        place = (target & 1) * (cols // 2) + (target >> 1)
-        row = pl.multiple_of(place * block, block)
-        column = pl.multiple_of(source_ref[level, q] * block, block)
-        acc[pl.ds(row, block), pl.ds(column, block)] += panel_ref[0, 0, q].astype(jnp.float32)
-        return carry
-
-    lax.fori_loop(0, tiles, add, 0)
-    out_ref[0] = acc[...].astype(out_ref.dtype)
-
-
-def fold(panels, tile_source, tile_target, rows, cols):
-    levels, _, tiles, block, _ = panels.shape
-    return pl.pallas_call(
-        functools.partial(fold_kernel, rows, cols),
-        out_shape=jax.ShapeDtypeStruct((levels, cols * block, rows * block), jnp.bfloat16),
-        grid_spec=pltpu.PrefetchScalarGridSpec(
-            num_scalar_prefetch=2,
-            grid=(levels,),
-            in_specs=[pl.BlockSpec((1, 1, tiles, block, block), lambda s, *_: (s, 0, 0, 0, 0))],
-            out_specs=pl.BlockSpec((1, cols * block, rows * block), lambda s, *_: (s, 0, 0)),
-            scratch_shapes=[pltpu.VMEM((cols * block, rows * block), jnp.float32)],
-        ),
-        compiler_params=pltpu.CompilerParams(vmem_limit_bytes=56 * 1024 * 1024),
-    )(tile_source[:, 0], tile_target[:, 0], panels)
-
-
-def solve_kernel(rows, cols, window, right_ref, diag_ref, matrix_ref, out_ref,
-                 matrix, gathered, pair_out, pair_in, own, shard_out, shard_in,
-                 matrix_sem, gather_send, gather_recv, pair_send, pair_recv, shard_send, shard_recv):
+def fold_links(tile_source, tile_target, rows, cols):
+    tiles = tile_source.shape[1]
+    place = (tile_target & 1) * (cols // 2) + (tile_target >> 1)
+    key = place * rows + tile_source
+    position = jnp.arange(tiles, dtype=jnp.int32)
+    pairs = rows * cols
+    want = jnp.concatenate([key, jnp.broadcast_to(jnp.arange(pairs, dtype=jnp.int32), (key.shape[0], pairs))], axis=1)
+    limit = jnp.concatenate([position, jnp.full((pairs,), tiles, jnp.int32)])
+    hit = (want[:, :, None] == key[:, None, :]) & (position[None, None, :] < limit[None, :, None])
+    last = jnp.max(jnp.where(hit, position[None, None, :], -1), axis=2)
+    return jnp.where(last < 0, tiles, last)
+
+
+def solve_kernel(rows, cols, link_ref, right_ref, diag_ref, panel_ref, out_ref,
+                 panels, runs, matrix, gathered, pair_out, pair_in, own, shard_out, shard_in,
+                 panel_sem, gather_send, gather_recv, pair_send, pair_recv, shard_send, shard_recv):
     sections, block, width = right_ref.shape
     levels = sections - 1
+    tiles = panels.shape[1]
     halves = gathered.shape[1]
     part = width // halves
     chips = cols // 2
@@ -63,9 +44,9 @@
     sibling = (i, z * 2 + 1 - core)
 
     def load(s):
-        return pltpu.make_async_copy(matrix_ref.at[s], matrix.at[s % window], matrix_sem.at[s % window])
-
-    for s in range(min(window, levels)):
+        return pltpu.make_async_copy(panel_ref.at[s, 0], panels.at[s], panel_sem.at[s])
+
+    for s in range(levels):
         load(s).start()
 
     barrier = pltpu.get_barrier_semaphore()
@@ -118,9 +99,9 @@
         other = pl.ds(pl.multiple_of((1 - core) * tall, tall), tall)
         mine = pl.ds(pl.multiple_of(core * tall, tall), tall)
         pair_out[p, h] = jnp.dot(
-            matrix[s % window, other, :], segment, preferred_element_type=jnp.float32).astype(jnp.bfloat16)
+            matrix[s % 2, other, :], segment, preferred_element_type=jnp.float32).astype(jnp.bfloat16)
         pair_copy(p, h).start()
-        own[h] = jnp.dot(matrix[s % window, mine, :], segment, preferred_element_type=jnp.float32)
+        own[h] = jnp.dot(matrix[s % 2, mine, :], segment, preferred_element_type=jnp.float32)
 
     def combine(s, h):
         p = s % 2
@@ -148,16 +129,26 @@
         for d in range(1, chips):
             shard_copy(p, h, d).wait_send()
 
+    def fold(s):
+        load(s).wait()
+
+        def add(q, carry):
+            runs[q] = panels[s, q].astype(jnp.float32) + runs[link_ref[s, q]]
+            return carry
+
+        def place(k, carry):
+            matrix[s % 2, block_of(k // rows), block_of(k % rows)] = runs[link_ref[s, tiles + k]].astype(jnp.bfloat16)
+            return carry
+
+        lax.fori_loop(0, tiles, add, 0, unroll=2)
+        lax.fori_loop(0, rows * cols, place, 0, unroll=4)
+
     def advance(s, last):
-        load(s).wait()
         for h in range(halves):
             update(s, h)
-        for h in range(halves):
             combine(s, h)
-        if window < levels and not last:
-            @pl.when(s + window < levels)
-            def _():
-                load(s + window).start()
+        if not last:
+            fold(s + 1)
         for h in range(halves):
             segment = finish(s + 1, h, incoming_of(s, h))
             if not last:
@@ -167,6 +158,8 @@
 
     for h in range(halves):
         spread(0, h, finish(0, h, None))
+    runs[tiles] = jnp.zeros((block, block), jnp.float32)
+    fold(0)
 
     def step(s, carry):
         advance(s, False)
@@ -183,24 +176,26 @@
     halves = 2 if width % 256 == 0 else 1
     part = width // halves
     chips = cols // 2
-    matrix = fold(panels, tile_source, tile_target, rows, cols)
-    window = levels if levels * matrix[0].size * 2 <= 24 * 1024 * 1024 else 2
+    tiles = panels.shape[2]
+    links = fold_links(tile_source[:, 0], tile_target[:, 0], rows, cols)
     dma = pltpu.SemaphoreType.DMA
     vmem = pl.BlockSpec(memory_space=pltpu.VMEM)
     solved = pl.pallas_call(
-        functools.partial(solve_kernel, rows, cols, window),
+        functools.partial(solve_kernel, rows, cols),
         out_shape=jax.ShapeDtypeStruct((sections, block, width), jnp.float32),
-        in_specs=[vmem, vmem, pl.BlockSpec(memory_space=pl.ANY)],
+        in_specs=[pl.BlockSpec(memory_space=pltpu.SMEM), vmem, vmem, pl.BlockSpec(memory_space=pl.ANY)],
         out_specs=vmem,
         scratch_shapes=[
-            pltpu.VMEM((window, cols * block, rows * block), jnp.bfloat16),
+            pltpu.VMEM((levels, tiles, block, block), jnp.bfloat16),
+            pltpu.VMEM((tiles + 1, block, block), jnp.float32),
+            pltpu.VMEM((2, cols * block, rows * block), jnp.bfloat16),
             pltpu.VMEM((2, halves, rows * block, part), jnp.bfloat16),
             pltpu.VMEM((2, halves, chips * block, part), jnp.bfloat16),
             pltpu.VMEM((2, halves, chips * block, part), jnp.bfloat16),
             pltpu.VMEM((halves, chips * block, part), jnp.float32),
             pltpu.VMEM((2, halves, chips * block, part), jnp.bfloat16),
             pltpu.VMEM((2, halves, chips - 1, block, part), jnp.bfloat16),
-            dma((window,)),
+            dma((levels,)),
             dma((2, halves, rows - 1)),
             dma((2, halves, rows - 1)),
             dma((2, halves)),
@@ -210,7 +205,7 @@
         ],
         compiler_params=pltpu.CompilerParams(
             collective_id=0, has_side_effects=True, vmem_limit_bytes=56 * 1024 * 1024),
-    )(right_side[0, 0], diag_inverse[0, 0], matrix)
+    )(links, right_side[0, 0], diag_inverse[0, 0], panels)
     return solved[None, None]
 
 

time: 110 us -> 85.3 us (0.78)
  Pallas kernels: 106 us -> 80.6 us
  other arithmetic: 0 us -> 2.18 us
  local copies, waits for them, and re-layouts: 3.57 us -> 2.28 us
    pallas_call x2 -> x1, Pallas kernels: 106 us -> 80.6 us  [local(): pl.pallas_call(functools.partial(solve_kernel, rows, cols), out_shape=jax...]
    unnamed x2, local copies, waits for them, and re-layouts: 3.57 us -> 2.27 us
where the time goes in v2:
time: 85.3 us; the launch traced here: 85.1 us
  Pallas kernels  80.6 us (94%)
  local copies, waits for them, and re-layouts  2.28 us (3%)
  other arithmetic  2.18 us (3%)
    pallas_call x1, Pallas kernels, local(): pl.pallas_call(functools.partial(solve_kernel, rows, cols), out_shape=jax...  80.6 us
    unnamed x2, local copies, waits for them, and re-layouts  2.27 us

profile of v2, /device:TPU:0, one launch (start us, length us, event | category | flops | bytes accessed | tf_op | source)
XLA Modules:
  0.0 85.1 jit_solution(13923004065984518138)
XLA Ops:
  0.0 0.7 multiply_add_fusion
  0.7 0.1 pad_add_fusion
  0.8 0.7 iota_compare_fusion
  1.5 0.1 select_reduce_fusion
  1.6 0.6 compare_select_fusion.link_ref
  2.2 80.6 %shard_map.55 = f32[8,128,256]{2,1,0:T(8,128)} custom-call(s32[7,82]{1,0:T(8,128)} %compare_select_fusion.link_ref, bf16[8,128,256]{2,1,0:T(8,128)(2,1)} %bitcast.7, bf16[8,128,128]{2,1,0:T(8,128)(2,1)} %bitcast.8, bf16[7,1,50,128,128]{4,3,2,1,0:T(8,128)(2,1)} %panel_ref.1), custom_call_target="tpu_custom_call" | custom-call | tf_op jit(solution)/shard_map/pallas_call | solution.py:183
  82.8 2.3 %copy.10 = f32[1,1,8,128,256]{4,3,2,1,0:T(8,128)} copy(f32[1,1,8,128,256]{4,3,2,1,0:T(8,128)} %bitcast.6) | data formatting | bytes 2097152
  (2 shorter events, 0.0 us)
